TPU v7x, 16 devices: a whole 2x2x2 slice. The times are simulated.
16 devices in a mesh: rep: 1, dp: 16 (over x, y, z, core).
Axes of the slice: x: 2, y: 2, z: 2, core: 2. Of those that a mesh axis runs over, the one named last changes fastest.
Arguments:
- g_w_gate: bfloat16 [16, 2, 896, 2560], P(('rep', 'dp'))
- g_w_up: bfloat16 [16, 2, 896, 2560], P(('rep', 'dp'))
- g_w_down: bfloat16 [16, 2, 2560, 896], P(('rep', 'dp'))
- w_gate: bfloat16 [2, 896, 2560], replicated
- w_up: bfloat16 [2, 896, 2560], replicated
- w_down: bfloat16 [2, 2560, 896], replicated
- m_w_gate: float32 [2, 896, 2560], P(None, 'dp')
- m_w_up: float32 [2, 896, 2560], P(None, 'dp')
- m_w_down: float32 [2, 2560, 896], P(None, 'dp')
- v_w_gate: float32 [2, 896, 2560], P(None, 'dp')
- v_w_up: float32 [2, 896, 2560], P(None, 'dp')
- v_w_down: float32 [2, 2560, 896], P(None, 'dp')
Outputs:
- output 1: bfloat16 [2, 896, 2560], P('rep')
- output 2: bfloat16 [2, 896, 2560], P('rep')
- output 3: bfloat16 [2, 2560, 896], P('rep')
- output 4: float32 [2, 896, 2560], P('rep', 'dp')
- output 5: float32 [2, 896, 2560], P('rep', 'dp')
- output 6: float32 [2, 2560, 896], P('rep', 'dp')
- output 7: float32 [2, 896, 2560], P('rep', 'dp')
- output 8: float32 [2, 896, 2560], P('rep', 'dp')
- output 9: float32 [2, 2560, 896], P('rep', 'dp')
All inputs are finite; a program needn't handle non-finite values.
Results may differ from a plain program's by a relative error of at most 0.022.
Values are sent between devices in bfloat16 or wider.
A program may use at most 2 GiB of HBM per device.

v0:
```python
import jax
import jax.numpy as jnp
from jax import lax
from jax.experimental import pallas as pl
from jax.experimental.pallas import tpu as pltpu
from jax.sharding import PartitionSpec as P


MESH = pl.DeviceIdType.MESH
F32, BF16 = jnp.float32, jnp.bfloat16
N = 16
LAYERS = 2
TILES = 70
AXES = ((8, 4, 2), (4, 2, 8), (2, 8, 4))
SUB = 10
T = TILES // SUB
CHUNKS = LAYERS * SUB
TAIL = 4
LEAD = 2
LAG = 2
RING0 = 2 * LEAD + 2 + LAG
RING = 6
VM = pltpu.VMEM
ST1, ST2, ST3, AG3, AG2, AG1, ST0, AG0 = range(8)


def add_into(dst, *srcs):
    total = srcs[0][...].astype(F32)
    for one in srcs[1:]:
        total = total + one[...].astype(F32)
    dst[...] = total.astype(BF16)


def kernel(*refs):
    g, w, m, v = (refs[i : i + 3] for i in range(0, 12, 3))
    moments, new_w = refs[12:14]
    split, both, mate_part = refs[14:17]
    wo = [new_w.at[k] for k in range(3)]
    mo, vo = ([moments.at[i, k] for k in range(3)] for i in range(2))
    D, R1, R2, R3, O1, O2, O3, O4, W, s0r, rr, a0r, snd, ld, mv = refs[17:]
    me = lax.axis_index("dp")

    def bit(b):
        return lax.rem(me // b, 2)

    def flip(i, b):
        return i + b - 2 * b * bit(b)

    core = bit(1)
    mate = flip(me, 1)

    def remote(src, dst, send, recv, to):
        return pltpu.make_async_remote_copy(src, dst, send, recv, device_id={"dp": to}, device_id_type=MESH)

    def arrived(ref, sem):
        remote(ref, ref, snd.at[ST0, 0], sem, mate).wait_recv()

    def loaded(ref, sem):
        pltpu.make_async_copy(ref, ref, sem).wait()

    def where(ch):
        return ch // SUB, pl.ds(lax.rem(ch, SUB) * T, T)

    def owner(k, e1, e2, e3, c):
        b1, b2, b3 = AXES[k]
        return e1 * b1 + e2 * b2 + e3 * b3 + c

    def send_raw(ch):
        l, rows = where(ch)
        for half in range(2):
            for k in range(3):
                side = bit(AXES[k][0]) if half else 1 - bit(AXES[k][0])
                for q in range(4):
                    j = owner(k, side, q // 2, q % 2, 1 - core)
                    remote(g[k].at[l, j, rows], D.at[k, ch, 4 * side + q], snd.at[ST0, k], s0r.at[half, k, lax.rem(ch, RING0)], mate).start()

    def load_own(which, ch):
        l, rows = where(ch)
        slot = lax.rem(ch, 2)
        for k in range(3):
            b1, b2, b3 = AXES[k]
            m1, m2, m3 = bit(b1), bit(b2), bit(b3)
            if which == 0:
                for q in range(4):
                    j = owner(k, 1 - m1, q // 2, q % 2, core)
                    pltpu.make_async_copy(g[k].at[l, j, rows], O1.at[k, slot, q], ld.at[0, k, slot]).start()
            elif which == 1:
                for q in range(2):
                    j = owner(k, m1, 1 - m2, q, core)
                    pltpu.make_async_copy(g[k].at[l, j, rows], O2.at[k, slot, q], ld.at[1, k, slot]).start()
            elif which == 2:
                j = owner(k, m1, m2, 1 - m3, core)
                pltpu.make_async_copy(g[k].at[l, j, rows], O3.at[k, slot], ld.at[2, k, slot]).start()
            else:
                pltpu.make_async_copy(g[k].at[l, me, rows], O4.at[k, slot], ld.at[3, k, slot]).start()
                pltpu.make_async_copy(w[k].at[l, me, rows], W.at[k, slot], ld.at[4, k, slot]).start()

    def stage1(ch):
        slot = lax.rem(ch, 2)
        for k in range(3):
            b1, _, _ = AXES[k]
            base = 4 * (1 - bit(b1))
            arrived(D.at[k, ch, pl.ds(base, 4)], s0r.at[0, k, lax.rem(ch, RING0)])
            loaded(O1.at[k, slot], ld.at[0, k, slot])

            def one(q, _):
                add_into(D.at[k, ch, base + q], O1.at[k, slot, q], D.at[k, ch, base + q])
                return 0

            lax.fori_loop(0, 4, one, 0)
            remote(D.at[k, ch, pl.ds(base, 4)], R1.at[k, ch], snd.at[ST1, k], rr.at[ST1, k, lax.rem(ch, RING)], flip(me, b1)).start()

    def stage2(ch):
        slot, ring = lax.rem(ch, 2), lax.rem(ch, RING)
        for k in range(3):
            b1, b2, _ = AXES[k]
            half = 2 * (1 - bit(b2))
            base = 4 * bit(b1) + half
            arrived(D.at[k, ch, pl.ds(4 * bit(b1), 4)], s0r.at[1, k, lax.rem(ch, RING0)])
            arrived(R1.at[k, ch], rr.at[ST1, k, ring])
            loaded(O2.at[k, slot], ld.at[1, k, slot])

            def one(q, _):
                add_into(D.at[k, ch, base + q], O2.at[k, slot, q], D.at[k, ch, base + q], R1.at[k, ch, half + q])
                return 0

            lax.fori_loop(0, 2, one, 0)
            remote(D.at[k, ch, pl.ds(base, 2)], R2.at[k, ch], snd.at[ST2, k], rr.at[ST2, k, ring], flip(me, b2)).start()

    def stage3(ch):
        slot, ring = lax.rem(ch, 2), lax.rem(ch, RING)
        for k in range(3):
            b1, b2, b3 = AXES[k]
            m1, m2, n3 = bit(b1), bit(b2), 1 - bit(b3)
            mine = D.at[k, ch, 4 * m1 + 2 * m2 + n3]
            arrived(R2.at[k, ch], rr.at[ST2, k, ring])
            loaded(O3.at[k, slot], ld.at[2, k, slot])
            add_into(mine, O3.at[k, slot], mine, R1.at[k, ch, 2 * m2 + n3], R2.at[k, ch, n3])
            remote(mine, R3.at[k, ch], snd.at[ST3, k], rr.at[ST3, k, ring], flip(me, b3)).start()

    def give(k, ch, stage, blocks, to):
        l, rows = where(ch)
        recv = a0r.at[k, lax.min(ch // TAIL, 1)] if stage == AG0 else rr.at[stage, k, lax.rem(ch, RING)]
        for j in blocks:
            part = wo[k].at[l, j, rows]
            remote(part, part, snd.at[stage, k], recv, to).start()

    def update(ch):
        l, rows = where(ch)
        slot, ring = lax.rem(ch, 2), lax.rem(ch, RING)

        @pl.when(ch == 0)
        def _():
            for k in range(3):
                loaded(mo[k], mv.at[0, k])
                loaded(vo[k], mv.at[1, k])

        for k in range(3):
            b1, b2, b3 = AXES[k]
            m1, m2, m3 = bit(b1), bit(b2), bit(b3)
            arrived(R3.at[k, ch], rr.at[ST3, k, ring])
            loaded(O4.at[k, slot], ld.at[3, k, slot])
            loaded(W.at[k, slot], ld.at[4, k, slot])
            total = O4[k, slot].astype(F32)
            for one in (D.at[k, ch, 4 * m1 + 2 * m2 + m3], R1.at[k, ch, 2 * m2 + m3], R2.at[k, ch, m3], R3.at[k, ch]):
                total = total + one[...].astype(F32)
            grad = total.astype(BF16).astype(F32)
            new_m = 0.9 * mo[k][l, rows] + 0.1 * grad
            new_v = 0.95 * vo[k][l, rows] + 0.05 * grad * grad
            old = W[k, slot].astype(F32)
            mo[k][l, rows] = new_m
            vo[k][l, rows] = new_v
            wo[k][l, me, rows] = (old - 0.02 * (new_m * lax.rsqrt(new_v + 1e-8) + 0.1 * old)).astype(BF16)
            give(k, ch, AG3, (me,), flip(me, b3))
            give(k, ch, AG0, (me,), mate)

    def double3(ch):
        l, rows = where(ch)
        for k in range(3):
            _, b2, b3 = AXES[k]
            got = flip(me, b3)
            arrived(wo[k].at[l, got, rows], rr.at[AG3, k, lax.rem(ch, RING)])
            give(k, ch, AG2, (me, got), flip(me, b2))
            give(k, ch, AG0, (got,), mate)

    def double2(ch):
        l, rows = where(ch)
        for k in range(3):
            b1, b2, b3 = AXES[k]
            held = (me, flip(me, b3))
            got = tuple(flip(j, b2) for j in held)
            arrived(wo[k].at[l, pl.ds(0, 2), rows], rr.at[AG2, k, lax.rem(ch, RING)])
            give(k, ch, AG0, got, mate)

            @pl.when(ch >= TAIL)
            def _():
                give(k, ch, AG1, held + got, flip(me, b1))


    def double1(ch):
        l, rows = where(ch)
        for k in range(3):
            b1, b2, b3 = AXES[k]
            held = (me, flip(me, b3))
            got = tuple(flip(j, b1) for j in held + tuple(flip(j, b2) for j in held))
            arrived(wo[k].at[l, pl.ds(0, 4), rows], rr.at[AG1, k, lax.rem(ch, RING)])

            @pl.when(ch < CHUNKS - 1)
            def _():
                give(k, ch, AG0, got, mate)

            @pl.when(ch == CHUNKS - 1)
            def _():
                for q in range(4):
                    mate_part[k, q] = wo[k][l, owner(k, 1 - bit(b1), q // 2, q % 2, core), rows]

    def take_late():
        late = pl.ds(0, TAIL * T)
        for k in range(3):
            arrived(R1.at[k, pl.ds(0, TAIL)], a0r.at[k, 0])

            @pl.when(core == k - 1 if k else core >= 0)
            def _():
                def one(q, _):
                    if k:
                        split[q] = wo[k][0, owner(k, bit(AXES[k][0]), q // 4, lax.rem(q // 2, 2), lax.rem(q, 2)), late]
                    else:
                        both[q] = wo[k][0, owner(k, bit(AXES[k][0]), q // 2, lax.rem(q, 2), core), late]
                    return 0

                lax.fori_loop(0, 8 if k else 4, one, 0)

    load_own(0, 0)
    for k in range(3):
        pltpu.make_async_copy(m[k], mo[k], mv.at[0, k]).start()
        pltpu.make_async_copy(v[k], vo[k], mv.at[1, k]).start()

    barrier = pltpu.get_barrier_semaphore()
    for b in (1, 2, 4, 8):
        pl.semaphore_signal(barrier, inc=1, device_id={"dp": flip(me, b)}, device_id_type=MESH)
    pl.semaphore_wait(barrier, 4)

    for ch in range(LEAD):
        send_raw(ch)

    def step(s, _):
        def at(lag, do, *args, start=0):
            ch = s - lag

            @pl.when((ch >= start) & (ch < CHUNKS))
            def _():
                do(*args, ch)

        at(0, stage1)
        at(-LEAD, send_raw)
        at(-1, load_own, 0)
        at(LAG - 1, load_own, 1)
        at(LAG, load_own, 2)
        at(LAG + 1, load_own, 3)
        at(LAG, stage2)
        at(LAG + 1, stage3)
        at(LAG + 2, update)
        at(LAG + 3, double3)
        at(LAG + 4, double2)
        at(LAG + 5, double1, start=TAIL)
        pl.when(s == CHUNKS)(take_late)
        return 0

    lax.fori_loop(0, CHUNKS + LAG + 5, step, 0)

    for k in range(3):
        arrived(wo[k].at[:, pl.ds(0, 7), pl.ds(0, 62)], a0r.at[k, 1])

    for k in range(3):
        for stage, sent in (
            (ST0, D.at[k]),
            (ST1, R1.at[k]),
            (ST2, R2.at[k]),
            (ST3, R3.at[k]),
            (AG3, wo[k].at[:, pl.ds(0, 1)]),
            (AG2, wo[k].at[:, pl.ds(0, 2)]),
            (AG1, R1.at[k, pl.ds(0, CHUNKS - TAIL)]),
            (AG0, D.at[k, :, pl.ds(0, 7)]),
        ):
            remote(sent, sent, snd.at[stage, k], a0r.at[k, 0], mate).wait_send()


def run_copies(pairs, sem):
    copies = [pltpu.make_async_copy(one, other, sem.at[i]) for i, (one, other) in enumerate(pairs)]
    for copy in copies:
        copy.start()
    for copy in copies:
        copy.wait()


def late_blocks(k, far):
    b1, b2, b3 = AXES[k]
    side = lax.rem(lax.axis_index("dp") // b1, 2)
    side = 1 - side if far else side
    return [side * b1 + q // 4 * b2 + q // 2 % 2 * b3 + q % 2 for q in range(8)]


def write_early(moments, new_w, *refs):
    *targets, sem = refs
    late = pl.ds(0, TAIL * T)
    pairs = []
    for k in range(3):
        rest = pl.ds(TAIL * T, TILES - TAIL * T)
        pairs += [(new_w.at[k, 1], targets[k].at[1]), (new_w.at[k, 0, :, rest], targets[k].at[0, :, rest])]
        pairs += [(new_w.at[k, 0, j, late], targets[k].at[0, j, late]) for j in late_blocks(k, False)]
    pairs += [(moments.at[i, k], targets[3 + 3 * i + k]) for i in range(2) for k in range(3)]
    run_copies(pairs, sem)


def put_late(split, both, targets, core, other, sem, more=()):
    late = pl.ds(0, TAIL * T)
    far = late_blocks(0, True)
    pairs = [*more] + [(both.at[q], targets[0].at[0, far[2 * q] + other, late]) for q in range(4)]
    for k in (1, 2):

        @pl.when(core == k - 1)
        def _():
            run_copies(pairs + [(split.at[q], targets[k].at[0, j, late]) for q, j in enumerate(late_blocks(k, True))], sem)


def write_next(*refs):
    split, both, targets, sem = refs[0], refs[1], refs[5:8], refs[8]
    core = lax.rem(lax.axis_index("dp"), 2)
    put_late(split, both, targets, core, core, sem)


def write_last(*refs):
    split, both, last, targets, sem = refs[0], refs[1], refs[2], refs[6:9], refs[9]
    core = lax.rem(lax.axis_index("dp"), 2)
    end, more = pl.ds(TILES - T, T), []
    for k in range(3):
        far = late_blocks(k, True)
        more += [(last.at[k, q], targets[k].at[1, far[2 * q] + 1 - core, end]) for q in range(4)]
    put_late(split, both, targets, 1 - core, 1 - core, sem, more)


def tiled(a, parts):
    rows, columns = a.shape[1] // parts // 8, a.shape[2] // 128
    a = a.reshape(LAYERS, parts, rows, 8, columns, 128).transpose(0, 1, 2, 4, 3, 5)
    return a.reshape(LAYERS, parts, TILES, 16, 128)


def untiled(a, shape):
    rows, columns = shape[1] // a.shape[1] // 8, shape[2] // 128
    a = a.reshape(LAYERS, a.shape[1], rows, columns, 8, 128).transpose(0, 1, 2, 4, 3, 5)
    return a.reshape(shape)


def solution(mesh):
    def step(*arrays):
        terms, weights, m, v = (arrays[i : i + 3] for i in (0, 3, 6, 9))
        whole, part = (LAYERS, N, TILES, 16, 128), (LAYERS, TILES, 16, 128)
        block = (T, 16, 128)
        dma = pltpu.SemaphoreType.DMA
        new = pl.pallas_call(
            kernel,
            out_shape=[VM((2, 3, *part), F32), VM((3, *whole), BF16)] + [VM((8, TAIL * T, 16, 128), BF16), VM((4, TAIL * T, 16, 128), BF16), VM((3, 4, *block), BF16)],
            in_specs=[pl.BlockSpec(memory_space=pltpu.HBM)] * 12,
            out_specs=[pl.BlockSpec(memory_space=pltpu.VMEM)] * 5,
            scratch_shapes=[
                pltpu.VMEM((3, CHUNKS, 8, *block), BF16),
                pltpu.VMEM((3, CHUNKS, 4, *block), BF16),
                pltpu.VMEM((3, CHUNKS, 2, *block), BF16),
                pltpu.VMEM((3, CHUNKS, *block), BF16),
                pltpu.VMEM((3, 2, 4, *block), BF16),
                pltpu.VMEM((3, 2, 2, *block), BF16),
                pltpu.VMEM((3, 2, *block), BF16),
                pltpu.VMEM((3, 2, *block), BF16),
                pltpu.VMEM((3, 2, *block), BF16),
                dma((2, 3, RING0)),
                dma((6, 3, RING)),
                dma((3, 2)),
                dma((8, 3)),
                dma((5, 3, 2)),
                dma((2, 3)),
            ],
            compiler_params=pltpu.CompilerParams(collective_id=0, has_side_effects=True, vmem_limit_bytes=28 * 2**20),
            name="sum_step_gather",
        )(
            *(tiled(t[0], N) for t in terms),
            *(tiled(one, N) for one in weights),
            *(tiled(one, 1)[:, 0] for one in (*m, *v)),
        )
        moments, new_w, split, both, last = new
        hbm, any_space, vmem = (pl.BlockSpec(memory_space=one) for one in (pltpu.HBM, pl.ANY, pltpu.VMEM))
        out_w, out_m = [jax.ShapeDtypeStruct(whole, BF16)] * 3, [jax.ShapeDtypeStruct(part, F32)] * 6

        def plain(body, out_shape, in_specs, copies, aliases, flops):
            return pl.pallas_call(
                body,
                out_shape=out_shape,
                in_specs=in_specs,
                out_specs=[hbm] * len(out_shape),
                scratch_shapes=[dma((copies,))],
                input_output_aliases=aliases,
                compiler_params=pltpu.CompilerParams(vmem_limit_bytes=2**20),
                cost_estimate=pl.CostEstimate(flops=flops, bytes_accessed=flops // 100, transcendentals=0),
            )

        split = lax.ppermute(split, "dp", [(i, i ^ (AXES[2][0] if i % 2 else AXES[1][0])) for i in range(N)])
        both = lax.ppermute(both, "dp", [(i, i ^ AXES[0][0]) for i in range(N)])
        last = lax.ppermute(last, "dp", [(i, i ^ 1) for i in range(N)])
        *new_w, m0, m1, m2, v0, v1, v2 = plain(write_early, out_w + out_m, [vmem] * 2, 36, {}, 2 * 10**9)(moments, new_w)
        *new_w, split, both = lax.optimization_barrier((*new_w, split, both))
        mates = [lax.ppermute(one, "dp", [(i, i ^ 1) for i in range(N)]) for one in (split, both)]
        new_w = plain(write_next, out_w, [any_space] * 2 + [hbm] * 3, 12, {2: 0, 3: 1, 4: 2}, 10**9)(split, both, *new_w)
        new_w = plain(write_last, out_w, [any_space] * 3 + [hbm] * 3, 24, {3: 0, 4: 1, 5: 2}, 10**9)(*mates, last, *new_w)
        new = (*new_w, m0, m1, m2, v0, v1, v2)
        return (
            *(untiled(one, w.shape) for one, w in zip(new[:3], weights, strict=True)),
            *(untiled(one[:, None], old.shape) for one, old in zip(new[3:], (*m, *v), strict=True)),
        )

    all_of, cut = P(None, None, None), P(None, "dp", None)
    return jax.shard_map(
        step,
        mesh=mesh,
        in_specs=(P(("rep", "dp"), None, None, None),) * 3 + (all_of,) * 3 + (cut,) * 6,
        out_specs=(P("rep", None, None),) * 3 + (P("rep", "dp", None),) * 6,
        check_vma=False,
    )
```

profile of v0, /device:TPU:0, one launch (start us, length us, event | category | flops | bytes accessed | tf_op | source)
XLA Modules:
  0.0 191.0 jit_solution(2028023338458523888)
XLA Ops:
  0.6 171.9 %sum_step_gather.1 = (f32[2,3,2,70,16,128]{5,4,3,2,1,0:T(8,128)S(1)}, bf16[3,2,16,70,16,128]{5,4,3,2,1,0:T(8,128)(2,1)S(1)}, bf16[8,28,16,128]{3,2,1,0:T(8,128)(...) custom-call(bf16[2,16,70,16,128]{4,3,2,1,0:T(8,128)(2,1)} %bitcast.108, ...), custom_call_target="tpu_custom_call" | custom-call | tf_op jit(solution)/shard_map/sum_step_gather/pallas_call | solution.py:360
  172.6 1.3 collective-permute-start
  173.8 0.8 collective-permute-start.1
  174.6 10.6 %shard_map.187 = (bf16[2,16,70,16,128]{4,3,2,1,0:T(8,128)(2,1)}, bf16[2,16,70,16,128]{4,3,2,1,0:T(8,128)(2,1)}, bf16[2,16,70,16,128]{4,3,2,1,0:T(8,128)(2,1)}, f...) custom-call(f32[2,3,2,70,16,128]{5,4,3,2,1,0:T(8,128)S(1)} %get-tupl, ...), custom_call_target="tpu_custom_call" | custom-call | flops 2000000000 | bytes 20000000 | tf_op jit(solution)/shard_map/pallas_call | solution.py:408
  185.3 0.5 collective-permute-done.1.refs_1_
  185.8 0.2 collective-permute-done.refs_0_
  186.0 0.0 collective-permute-start.2
  186.0 0.5 collective-permute-start.3
  186.5 0.0 collective-permute-start.4
  186.5 1.2 shard_map.188
  187.7 1.9 %collective-permute-done.4.refs_2_ = bf16[3,4,7,16,128]{4,3,2,1,0:T(8,128)(2,1)S(1)} collective-permute-done((bf16[3,4,7,16,128]{4,3,2,1,0:T(8,128)(2,1)S(1)}, bf16[3,4,7,16,128]{4,3,2,1,0:T(8,128)(2,1)S(1)}, u32[]{:S(2)}, u32[]{:S(2)}) %collective-permute-start.4) | collective-permute-done | bytes 344096 | tf_op jit(solution)/shard_map/ppermute | solution.py:407
  189.6 0.0 collective-permute-done.3.refs_1_
  189.6 0.0 collective-permute-done.2.refs_0_
  189.6 1.4 shard_map.189
Async XLA Ops:
  172.6 13.4 %collective-permute-start = (bf16[8,28,16,128]{3,2,1,0:T(8,128)(2,1)S(1)}, bf16[8,28,16,128]{3,2,1,0:T(8,128)(2,1)S(1)}, u32[]{:S(2)}, u32[]{:S(2)}) collective-permute-start(bf16[8,28,16,128]{3,2,1,0:T(8,128)(2,1)S(1)} %get-tuple-element.39), channel_id=1, source_target_pairs={{0,4},{1,3},{2,6},{3,1},{4,0},{5,7},{6,2},{7,5},{8,12},{9,11},{10,... | collective-permute-start | bytes 2752520 | tf_op jit(solution)/shard_map/ppermute | solution.py:405
  173.8 11.9 %collective-permute-start.1 = (bf16[4,28,16,128]{3,2,1,0:T(8,128)(2,1)S(1)}, bf16[4,28,16,128]{3,2,1,0:T(8,128)(2,1)S(1)}, u32[]{:S(2)}, u32[]{:S(2)}) collective-permute-start(bf16[4,28,16,128]{3,2,1,0:T(8,128)(2,1)S(1)} %get-tuple-element.40), channel_id=1, source_target_pairs={{0,8},{1,9},{2,10},{3,11},{4,12},{5,13},{6,14},{7,15},{8,0},{9,1},... | collective-permute-start | bytes 1376264 | tf_op jit(solution)/shard_map/ppermute | solution.py:406
  186.0 3.6 %collective-permute-start.2 = (bf16[8,28,16,128]{3,2,1,0:T(8,128)(2,1)S(1)}, bf16[8,28,16,128]{3,2,1,0:T(8,128)(2,1)S(1)}, u32[]{:S(2)}, u32[]{:S(2)}) collective-permute-start(bf16[8,28,16,128]{3,2,1,0:T(8,128)(2,1)S(1)} %collective-permute-done.refs_0_), channel_id=1, source_target_pairs={{0,1},{1,0},{2,3},{3,2},{4,5},{5,4},{6,7},{7,6},{8,9},{9,8},{10,11... | collective-permute-start | bytes 2752520 | tf_op jit(solution)/shard_map/ppermute | solution.py:410
  186.0 3.6 %collective-permute-start.3 = (bf16[4,28,16,128]{3,2,1,0:T(8,128)(2,1)S(1)}, bf16[4,28,16,128]{3,2,1,0:T(8,128)(2,1)S(1)}, u32[]{:S(2)}, u32[]{:S(2)}) collective-permute-start(bf16[4,28,16,128]{3,2,1,0:T(8,128)(2,1)S(1)} %collective-permute-done.1.refs_1_), channel_id=1, source_target_pairs={{0,1},{1,0},{2,3},{3,2},{4,5},{5,4},{6,7},{7,6},{8,9},{9,8},{10,11... | collective-permute-start | bytes 1376264 | tf_op jit(solution)/shard_map/ppermute | solution.py:410
  186.5 3.1 %collective-permute-start.4 = (bf16[3,4,7,16,128]{4,3,2,1,0:T(8,128)(2,1)S(1)}, bf16[3,4,7,16,128]{4,3,2,1,0:T(8,128)(2,1)S(1)}, u32[]{:S(2)}, u32[]{:S(2)}) collective-permute-start(bf16[3,4,7,16,128]{4,3,2,1,0:T(8,128)(2,1)S(1)} %get-tuple-element.43), channel_id=1, source_target_pairs={{0,1},{1,0},{2,3},{3,2},{4,5},{5,4},{6,7},{7,6},{8,9},{9,8},{10,11... | collective-permute-start | bytes 1032200 | tf_op jit(solution)/shard_map/ppermute | solution.py:407
where the time goes:
time: 191 us
  Pallas kernels  185 us (97%)
  waiting for transfers between devices  2.69 us (1%)
  starting transfers between devices  2.57 us (1%)
    pallas_call x1, Pallas kernels, step(): pl.pallas_call(kernel, out_shape=[VM((2, 3, *part), F32), VM((3, *whole),...  172 us
    pallas_call x1, Pallas kernels, step(): plain(write_early, out_w + out_m, [vmem] * 2, 36, {}, 2 * 10 ** 9)  10.6 us
  transfers between devices with their start and end apart: 5, of which 3 were waited for; matrix products, arithmetic and copies ran while one was open for 0% of the time, Pallas kernels for 6%

commit v1 on v0

v1 whole, which is shorter than its diff:
```python
import jax
import jax.numpy as jnp
from jax import lax
from jax.experimental import pallas as pl
from jax.experimental.pallas import tpu as pltpu
from jax.sharding import PartitionSpec as P


MESH = pl.DeviceIdType.MESH
F32, BF16 = jnp.float32, jnp.bfloat16
N = 16
LAYERS = 2
TILES = 70
AXES = ((8, 4, 2), (4, 2, 8), (2, 8, 4))
SUB = 10
T = TILES // SUB
CHUNKS = LAYERS * SUB
TAIL = 4
LEAD = 1
LAG = 1
RING = 4
VM = pltpu.VMEM
ST1, ST2, ST3, AG3, AG2, AG1, ST0, AG0 = range(8)


def add_into(dst, *srcs):
    total = srcs[0][...].astype(F32)
    for one in srcs[1:]:
        total = total + one[...].astype(F32)
    dst[...] = total.astype(BF16)


def kernel(*refs):
    g, w, m, v = (refs[i : i + 3] for i in range(0, 12, 3))
    moments, new_w = refs[12:14]
    split, both, mate_part = refs[14:17]
    wo = [new_w.at[k] for k in range(3)]
    mo, vo = ([moments.at[i, k] for k in range(3)] for i in range(2))
    D, R1, R2, R3, O1, O2, O3, O4, W, s0r, rr, a0r, snd, ld, mv = refs[17:]
    me = lax.axis_index("dp")

    def bit(b):
        return lax.rem(me // b, 2)

    def flip(i, b):
        return i + b - 2 * b * bit(b)

    core = bit(1)
    mate = flip(me, 1)

    def remote(src, dst, send, recv, to):
        return pltpu.make_async_remote_copy(src, dst, send, recv, device_id={"dp": to}, device_id_type=MESH)

    def arrived(ref, sem):
        remote(ref, ref, snd.at[ST0], sem, mate).wait_recv()

    def loaded(ref, sem):
        pltpu.make_async_copy(ref, ref, sem).wait()

    def where(ch):
        return ch // SUB, pl.ds(lax.rem(ch, SUB) * T, T)

    def owner(k, e1, e2, e3, c):
        b1, b2, b3 = AXES[k]
        return e1 * b1 + e2 * b2 + e3 * b3 + c

    def send_raw(ch):
        l, rows = where(ch)
        for half in range(2):
            for k in range(3):
                side = bit(AXES[k][0]) if half else 1 - bit(AXES[k][0])
                for q in range(4):
                    j = owner(k, side, q // 2, q % 2, 1 - core)
                    sem = s0r.at[3 if half else k, lax.rem(ch, RING)]
                    remote(g[k].at[l, j, rows], D.at[k, ch, 4 * side + q], snd.at[ST0], sem, mate).start()

    def load_own(which, ch):
        l, rows = where(ch)
        slot = lax.rem(ch, 2)
        for k in range(3):
            b1, b2, b3 = AXES[k]
            m1, m2, m3 = bit(b1), bit(b2), bit(b3)
            if which == 0:
                for q in range(4):
                    j = owner(k, 1 - m1, q // 2, q % 2, core)
                    pltpu.make_async_copy(g[k].at[l, j, rows], O1.at[slot, k, q], ld.at[0, slot]).start()
            elif which == 1:
                for q in range(2):
                    j = owner(k, m1, 1 - m2, q, core)
                    pltpu.make_async_copy(g[k].at[l, j, rows], O2.at[slot, k, q], ld.at[1, slot]).start()
            elif which == 2:
                j = owner(k, m1, m2, 1 - m3, core)
                pltpu.make_async_copy(g[k].at[l, j, rows], O3.at[slot, k], ld.at[2, slot]).start()
            else:
                pltpu.make_async_copy(g[k].at[l, me, rows], O4.at[slot, k], ld.at[3, slot]).start()
                pltpu.make_async_copy(w[k].at[l, me, rows], W.at[slot, k], ld.at[4, slot]).start()

    def stage1(ch):
        slot, ring = lax.rem(ch, 2), lax.rem(ch, RING)
        loaded(O1.at[slot], ld.at[0, slot])
        for k in range(3):
            b1, _, _ = AXES[k]
            base = 4 * (1 - bit(b1))
            arrived(D.at[k, ch, pl.ds(base, 4)], s0r.at[k, ring])

            def one(q, _):
                add_into(D.at[k, ch, base + q], O1.at[slot, k, q], D.at[k, ch, base + q])
                return 0

            lax.fori_loop(0, 4, one, 0)
            remote(D.at[k, ch, pl.ds(base, 4)], R1.at[ch, k], snd.at[ST1], rr.at[ST1, ring], flip(me, b1)).start()

    def stage2(ch):
        slot, ring = lax.rem(ch, 2), lax.rem(ch, RING)
        arrived(R1.at[ch], s0r.at[3, ring])
        arrived(R1.at[ch], rr.at[ST1, ring])
        loaded(O2.at[slot], ld.at[1, slot])
        for k in range(3):
            b1, b2, _ = AXES[k]
            half = 2 * (1 - bit(b2))
            base = 4 * bit(b1) + half

            def one(q, _):
                add_into(D.at[k, ch, base + q], O2.at[slot, k, q], D.at[k, ch, base + q], R1.at[ch, k, half + q])
                return 0

            lax.fori_loop(0, 2, one, 0)
            remote(D.at[k, ch, pl.ds(base, 2)], R2.at[ch, k], snd.at[ST2], rr.at[ST2, ring], flip(me, b2)).start()

    def stage3(ch):
        slot, ring = lax.rem(ch, 2), lax.rem(ch, RING)
        arrived(R2.at[ch], rr.at[ST2, ring])
        loaded(O3.at[slot], ld.at[2, slot])
        for k in range(3):
            b1, b2, b3 = AXES[k]
            m1, m2, n3 = bit(b1), bit(b2), 1 - bit(b3)
            mine = D.at[k, ch, 4 * m1 + 2 * m2 + n3]
            add_into(mine, O3.at[slot, k], mine, R1.at[ch, k, 2 * m2 + n3], R2.at[ch, k, n3])
            remote(mine, R3.at[ch, k], snd.at[ST3], rr.at[ST3, ring], flip(me, b3)).start()

    def give(k, ch, stage, blocks, to):
        l, rows = where(ch)
        recv = a0r.at[lax.min(ch // TAIL, 1)] if stage == AG0 else rr.at[stage, lax.rem(ch, RING)]
        for j in blocks:
            part = wo[k].at[l, j, rows]
            remote(part, part, snd.at[stage], recv, to).start()

    def update(ch):
        l, rows = where(ch)
        slot, ring = lax.rem(ch, 2), lax.rem(ch, RING)

        @pl.when(ch == 0)
        def _():
            loaded(moments, mv.at[0])

        arrived(R3.at[ch], rr.at[ST3, ring])
        loaded(O4.at[slot], ld.at[3, slot])
        loaded(W.at[slot], ld.at[4, slot])
        for k in range(3):
            b1, b2, b3 = AXES[k]
            m1, m2, m3 = bit(b1), bit(b2), bit(b3)
            total = O4[slot, k].astype(F32)
            for one in (D.at[k, ch, 4 * m1 + 2 * m2 + m3], R1.at[ch, k, 2 * m2 + m3], R2.at[ch, k, m3], R3.at[ch, k]):
                total = total + one[...].astype(F32)
            grad = total.astype(BF16).astype(F32)
            new_m = 0.9 * mo[k][l, rows] + 0.1 * grad
            new_v = 0.95 * vo[k][l, rows] + 0.05 * grad * grad
            old = W[slot, k].astype(F32)
            mo[k][l, rows] = new_m
            vo[k][l, rows] = new_v
            wo[k][l, me, rows] = (old - 0.02 * (new_m * lax.rsqrt(new_v + 1e-8) + 0.1 * old)).astype(BF16)
            give(k, ch, AG3, (me,), flip(me, b3))
            give(k, ch, AG0, (me,), mate)

    def double3(ch):
        arrived(R3.at[ch], rr.at[AG3, lax.rem(ch, RING)])
        for k in range(3):
            _, b2, b3 = AXES[k]
            got = flip(me, b3)
            give(k, ch, AG2, (me, got), flip(me, b2))
            give(k, ch, AG0, (got,), mate)

    def double2(ch):
        arrived(R2.at[ch], rr.at[AG2, lax.rem(ch, RING)])
        for k in range(3):
            b1, b2, b3 = AXES[k]
            held = (me, flip(me, b3))
            got = tuple(flip(j, b2) for j in held)
            give(k, ch, AG0, got, mate)

            @pl.when(ch >= TAIL)
            def _():
                give(k, ch, AG1, held + got, flip(me, b1))


    def double1(ch):
        l, rows = where(ch)
        arrived(R1.at[ch], rr.at[AG1, lax.rem(ch, RING)])
        for k in range(3):
            b1, b2, b3 = AXES[k]
            held = (me, flip(me, b3))
            got = tuple(flip(j, b1) for j in held + tuple(flip(j, b2) for j in held))

            @pl.when(ch < CHUNKS - 1)
            def _():
                give(k, ch, AG0, got, mate)

            @pl.when(ch == CHUNKS - 1)
            def _():
                for q in range(4):
                    mate_part[k, q] = wo[k][l, owner(k, 1 - bit(b1), q // 2, q % 2, core), rows]

    def take_late():
        late = pl.ds(0, TAIL * T)
        arrived(R1.at[pl.ds(0, TAIL)], a0r.at[0])
        for k in range(3):

            @pl.when(core == k - 1 if k else core >= 0)
            def _():
                def one(q, _):
                    if k:
                        split[q] = wo[k][0, owner(k, bit(AXES[k][0]), q // 4, lax.rem(q // 2, 2), lax.rem(q, 2)), late]
                    else:
                        both[q] = wo[k][0, owner(k, bit(AXES[k][0]), q // 2, lax.rem(q, 2), core), late]
                    return 0

                lax.fori_loop(0, 8 if k else 4, one, 0)

    load_own(0, 0)
    for k in range(3):
        pltpu.make_async_copy(m[k], mo[k], mv.at[0]).start()
        pltpu.make_async_copy(v[k], vo[k], mv.at[0]).start()

    barrier = pltpu.get_barrier_semaphore()
    for b in (1, 2, 4, 8):
        pl.semaphore_signal(barrier, inc=1, device_id={"dp": flip(me, b)}, device_id_type=MESH)
    pl.semaphore_wait(barrier, 4)

    for ch in range(LEAD):
        send_raw(ch)

    def step(s, _):
        def at(lag, do, *args, start=0):
            ch = s - lag

            @pl.when((ch >= start) & (ch < CHUNKS))
            def _():
                do(*args, ch)

        at(0, stage1)
        at(-LEAD, send_raw)
        at(-1, load_own, 0)
        at(LAG - 1, load_own, 1)
        at(LAG, load_own, 2)
        at(LAG + 1, load_own, 3)
        at(LAG, stage2)
        at(LAG + 1, stage3)
        at(LAG + 2, update)
        at(LAG + 3, double3)
        at(LAG + 4, double2)
        at(LAG + 5, double1, start=TAIL)
        pl.when(s == CHUNKS)(take_late)
        return 0

    lax.fori_loop(0, CHUNKS + LAG + 5, step, 0)

    arrived(new_w.at[:, :, pl.ds(0, 7), pl.ds(0, 62)], a0r.at[1])
    for stage, sent in (
        (ST0, D),
        (ST1, R1),
        (ST2, R2),
        (ST3, R3),
        (AG3, R3),
        (AG2, R2),
        (AG1, R1.at[pl.ds(0, CHUNKS - TAIL)]),
        (AG0, D.at[:, :, pl.ds(0, 7)]),
    ):
        remote(sent, sent, snd.at[stage], a0r.at[0], mate).wait_send()


def run_copies(groups, sem):
    for i, (pairs, _) in enumerate(groups):
        for one, other in pairs:
            pltpu.make_async_copy(one, other, sem.at[i]).start()
    for i, (_, total) in enumerate(groups):
        pltpu.make_async_copy(total, total, sem.at[i]).wait()


def late_blocks(k, far):
    b1, b2, b3 = AXES[k]
    side = lax.rem(lax.axis_index("dp") // b1, 2)
    side = 1 - side if far else side
    return [side * b1 + q // 4 * b2 + q // 2 % 2 * b3 + q % 2 for q in range(8)]


def write_early(moments, new_w, *refs):
    *targets, sem = refs
    late, rest = pl.ds(0, TAIL * T), pl.ds(TAIL * T, TILES - TAIL * T)
    pairs = []
    for k in range(3):
        pairs += [(new_w.at[k, 1], targets[k].at[1]), (new_w.at[k, 0, :, rest], targets[k].at[0, :, rest])]
        pairs += [(new_w.at[k, 0, j, late], targets[k].at[0, j, late]) for j in late_blocks(k, False)]
    small = [(moments.at[i, k], targets[3 + 3 * i + k]) for i in range(2) for k in range(3)]
    run_copies([(pairs, new_w.at[:, :, :, pl.ds(0, TILES - TAIL * T // 4)]), (small, moments)], sem)


def put_late(split, both, targets, core, sem, more=()):
    late = pl.ds(0, TAIL * T)
    far = late_blocks(0, True)
    shared = ([(both.at[q], targets[0].at[0, far[2 * q] + core, late]) for q in range(4)], both)
    for k in (1, 2):

        @pl.when(core == k - 1)
        def _():
            run_copies([*more, shared, ([(split.at[q], targets[k].at[0, j, late]) for q, j in enumerate(late_blocks(k, True))], split)], sem)


def write_next(*refs):
    split, both, targets, sem = refs[0], refs[1], refs[5:8], refs[8]
    put_late(split, both, targets, lax.rem(lax.axis_index("dp"), 2), sem)


def write_last(*refs):
    split, both, last, targets, sem = refs[0], refs[1], refs[2], refs[6:9], refs[9]
    other = 1 - lax.rem(lax.axis_index("dp"), 2)
    end, ends = pl.ds(TILES - T, T), []
    for k in range(3):
        far = late_blocks(k, True)
        ends += [(last.at[k, q], targets[k].at[1, far[2 * q] + other, end]) for q in range(4)]
    put_late(split, both, targets, other, sem, [(ends, last)])


def tiled(a, parts):
    rows, columns = a.shape[1] // parts // 8, a.shape[2] // 128
    a = a.reshape(LAYERS, parts, rows, 8, columns, 128).transpose(0, 1, 2, 4, 3, 5)
    return a.reshape(LAYERS, parts, TILES, 16, 128)


def untiled(a, shape):
    rows, columns = shape[1] // a.shape[1] // 8, shape[2] // 128
    a = a.reshape(LAYERS, a.shape[1], rows, columns, 8, 128).transpose(0, 1, 2, 4, 3, 5)
    return a.reshape(shape)


def solution(mesh):
    def step(*arrays):
        terms, weights, m, v = (arrays[i : i + 3] for i in (0, 3, 6, 9))
        whole, part = (LAYERS, N, TILES, 16, 128), (LAYERS, TILES, 16, 128)
        block = (T, 16, 128)
        dma = pltpu.SemaphoreType.DMA
        new = pl.pallas_call(
            kernel,
            out_shape=[VM((2, 3, *part), F32), VM((3, *whole), BF16)] + [VM((8, TAIL * T, 16, 128), BF16), VM((4, TAIL * T, 16, 128), BF16), VM((3, 4, *block), BF16)],
            in_specs=[pl.BlockSpec(memory_space=pltpu.HBM)] * 12,
            out_specs=[pl.BlockSpec(memory_space=pltpu.VMEM)] * 5,
            scratch_shapes=[
                pltpu.VMEM((3, CHUNKS, 8, *block), BF16),
                pltpu.VMEM((CHUNKS, 3, 4, *block), BF16),
                pltpu.VMEM((CHUNKS, 3, 2, *block), BF16),
                pltpu.VMEM((CHUNKS, 3, *block), BF16),
                pltpu.VMEM((2, 3, 4, *block), BF16),
                pltpu.VMEM((2, 3, 2, *block), BF16),
                pltpu.VMEM((2, 3, *block), BF16),
                pltpu.VMEM((2, 3, *block), BF16),
                pltpu.VMEM((2, 3, *block), BF16),
                dma((4, RING)),
                dma((6, RING)),
                dma((2,)),
                dma((8,)),
                dma((5, 2)),
                dma((1,)),
            ],
            compiler_params=pltpu.CompilerParams(collective_id=0, has_side_effects=True, vmem_limit_bytes=28 * 2**20),
            name="sum_step_gather",
        )(
            *(tiled(t[0], N) for t in terms),
            *(tiled(one, N) for one in weights),
            *(tiled(one, 1)[:, 0] for one in (*m, *v)),
        )
        moments, new_w, split, both, last = new
        hbm, any_space, vmem = (pl.BlockSpec(memory_space=one) for one in (pltpu.HBM, pl.ANY, pltpu.VMEM))
        out_w, out_m = [jax.ShapeDtypeStruct(whole, BF16)] * 3, [jax.ShapeDtypeStruct(part, F32)] * 6

        def plain(body, out_shape, in_specs, semaphores, aliases, flops):
            return pl.pallas_call(
                body,
                out_shape=out_shape,
                in_specs=in_specs,
                out_specs=[hbm] * len(out_shape),
                scratch_shapes=[dma((semaphores,))],
                input_output_aliases=aliases,
                compiler_params=pltpu.CompilerParams(vmem_limit_bytes=2**20),
                cost_estimate=pl.CostEstimate(flops=flops, bytes_accessed=flops // 100, transcendentals=0),
            )

        split = lax.ppermute(split, "dp", [(i, i ^ (AXES[2][0] if i % 2 else AXES[1][0])) for i in range(N)])
        both = lax.ppermute(both, "dp", [(i, i ^ AXES[0][0]) for i in range(N)])
        last = lax.ppermute(last, "dp", [(i, i ^ 1) for i in range(N)])
        *new_w, m0, m1, m2, v0, v1, v2 = plain(write_early, out_w + out_m, [vmem] * 2, 2, {}, 2 * 10**9)(moments, new_w)
        *new_w, split, both = lax.optimization_barrier((*new_w, split, both))
        mates = [lax.ppermute(one, "dp", [(i, i ^ 1) for i in range(N)]) for one in (split, both)]
        new_w = plain(write_next, out_w, [any_space] * 2 + [hbm] * 3, 2, {2: 0, 3: 1, 4: 2}, 10**9)(split, both, *new_w)
        new_w = plain(write_last, out_w, [any_space] * 3 + [hbm] * 3, 3, {3: 0, 4: 1, 5: 2}, 10**9)(*mates, last, *new_w)
        new = (*new_w, m0, m1, m2, v0, v1, v2)
        return (
            *(untiled(one, w.shape) for one, w in zip(new[:3], weights, strict=True)),
            *(untiled(one[:, None], old.shape) for one, old in zip(new[3:], (*m, *v), strict=True)),
        )

    all_of, cut = P(None, None, None), P(None, "dp", None)
    return jax.shard_map(
        step,
        mesh=mesh,
        in_specs=(P(("rep", "dp"), None, None, None),) * 3 + (all_of,) * 3 + (cut,) * 6,
        out_specs=(P("rep", None, None),) * 3 + (P("rep", "dp", None),) * 6,
        check_vma=False,
    )
```

time: 191 us -> 190 us (level)
  Pallas kernels: 185 us -> 183 us
where the time goes in v1:
time: 190 us; the launch traced here: 189 us
  Pallas kernels  183 us (96%)
  waiting for transfers between devices  3.07 us (2%)
  starting transfers between devices  2.59 us (1%)
    pallas_call x1, Pallas kernels, step(): pl.pallas_call(kernel, out_shape=[VM((2, 3, *part), F32), VM((3, *whole),...  171 us
    pallas_call x1, Pallas kernels, step(): plain(write_early, out_w + out_m, [vmem] * 2, 2, {}, 2 * 10 ** 9)  10.3 us
  transfers between devices with their start and end apart: 5, of which 3 were waited for; matrix products, arithmetic and copies ran while one was open for 0% of the time, Pallas kernels for 6%

profile of v1, /device:TPU:0, one launch (start us, length us, event | category | flops | bytes accessed | tf_op | source)
XLA Modules:
  0.0 189.5 jit_solution(15533405705216297800)
XLA Ops:
  0.6 170.6 %sum_step_gather.1 = (f32[2,3,2,70,16,128]{5,4,3,2,1,0:T(8,128)S(1)}, bf16[3,2,16,70,16,128]{5,4,3,2,1,0:T(8,128)(2,1)S(1)}, bf16[8,28,16,128]{3,2,1,0:T(8,128)(...) custom-call(bf16[2,16,70,16,128]{4,3,2,1,0:T(8,128)(2,1)} %bitcast.108, ...), custom_call_target="tpu_custom_call" | custom-call | tf_op jit(solution)/shard_map/sum_step_gather/pallas_call | solution.py:351
  171.2 1.4 collective-permute-start
  172.7 0.6 collective-permute-start.1
  173.3 10.3 %shard_map.187 = (bf16[2,16,70,16,128]{4,3,2,1,0:T(8,128)(2,1)}, bf16[2,16,70,16,128]{4,3,2,1,0:T(8,128)(2,1)}, bf16[2,16,70,16,128]{4,3,2,1,0:T(8,128)(2,1)}, f...) custom-call(f32[2,3,2,70,16,128]{5,4,3,2,1,0:T(8,128)S(1)} %get-tupl, ...), custom_call_target="tpu_custom_call" | custom-call | flops 2000000000 | bytes 20000000 | tf_op jit(solution)/shard_map/pallas_call | solution.py:399
  183.6 0.7 collective-permute-done.1.refs_1_
  184.4 0.3 collective-permute-done.refs_0_
  184.7 0.0 collective-permute-start.2
  184.7 0.5 collective-permute-start.3
  185.2 0.0 collective-permute-start.4
  185.2 1.1 shard_map.188
  186.3 2.0 %collective-permute-done.4.refs_2_ = bf16[3,4,7,16,128]{4,3,2,1,0:T(8,128)(2,1)S(1)} collective-permute-done((bf16[3,4,7,16,128]{4,3,2,1,0:T(8,128)(2,1)S(1)}, bf16[3,4,7,16,128]{4,3,2,1,0:T(8,128)(2,1)S(1)}, u32[]{:S(2)}, u32[]{:S(2)}) %collective-permute-start.4) | collective-permute-done | bytes 344096 | tf_op jit(solution)/shard_map/ppermute | solution.py:398
  188.3 0.0 collective-permute-done.3.refs_1_
  188.3 0.0 collective-permute-done.2.refs_0_
  188.3 1.2 shard_map.189
Async XLA Ops:
  171.2 13.4 %collective-permute-start = (bf16[8,28,16,128]{3,2,1,0:T(8,128)(2,1)S(1)}, bf16[8,28,16,128]{3,2,1,0:T(8,128)(2,1)S(1)}, u32[]{:S(2)}, u32[]{:S(2)}) collective-permute-start(bf16[8,28,16,128]{3,2,1,0:T(8,128)(2,1)S(1)} %get-tuple-element.39), channel_id=1, source_target_pairs={{0,4},{1,3},{2,6},{3,1},{4,0},{5,7},{6,2},{7,5},{8,12},{9,11},{10,... | collective-permute-start | bytes 2752520 | tf_op jit(solution)/shard_map/ppermute | solution.py:396
  172.7 11.7 %collective-permute-start.1 = (bf16[4,28,16,128]{3,2,1,0:T(8,128)(2,1)S(1)}, bf16[4,28,16,128]{3,2,1,0:T(8,128)(2,1)S(1)}, u32[]{:S(2)}, u32[]{:S(2)}) collective-permute-start(bf16[4,28,16,128]{3,2,1,0:T(8,128)(2,1)S(1)} %get-tuple-element.40), channel_id=1, source_target_pairs={{0,8},{1,9},{2,10},{3,11},{4,12},{5,13},{6,14},{7,15},{8,0},{9,1},... | collective-permute-start | bytes 1376264 | tf_op jit(solution)/shard_map/ppermute | solution.py:397
  184.7 3.6 %collective-permute-start.2 = (bf16[8,28,16,128]{3,2,1,0:T(8,128)(2,1)S(1)}, bf16[8,28,16,128]{3,2,1,0:T(8,128)(2,1)S(1)}, u32[]{:S(2)}, u32[]{:S(2)}) collective-permute-start(bf16[8,28,16,128]{3,2,1,0:T(8,128)(2,1)S(1)} %collective-permute-done.refs_0_), channel_id=1, source_target_pairs={{0,1},{1,0},{2,3},{3,2},{4,5},{5,4},{6,7},{7,6},{8,9},{9,8},{10,11... | collective-permute-start | bytes 2752520 | tf_op jit(solution)/shard_map/ppermute | solution.py:401
  184.7 3.6 %collective-permute-start.3 = (bf16[4,28,16,128]{3,2,1,0:T(8,128)(2,1)S(1)}, bf16[4,28,16,128]{3,2,1,0:T(8,128)(2,1)S(1)}, u32[]{:S(2)}, u32[]{:S(2)}) collective-permute-start(bf16[4,28,16,128]{3,2,1,0:T(8,128)(2,1)S(1)} %collective-permute-done.1.refs_1_), channel_id=1, source_target_pairs={{0,1},{1,0},{2,3},{3,2},{4,5},{5,4},{6,7},{7,6},{8,9},{9,8},{10,11... | collective-permute-start | bytes 1376264 | tf_op jit(solution)/shard_map/ppermute | solution.py:401
  185.2 3.1 %collective-permute-start.4 = (bf16[3,4,7,16,128]{4,3,2,1,0:T(8,128)(2,1)S(1)}, bf16[3,4,7,16,128]{4,3,2,1,0:T(8,128)(2,1)S(1)}, u32[]{:S(2)}, u32[]{:S(2)}) collective-permute-start(bf16[3,4,7,16,128]{4,3,2,1,0:T(8,128)(2,1)S(1)} %get-tuple-element.43), channel_id=1, source_target_pairs={{0,1},{1,0},{2,3},{3,2},{4,5},{5,4},{6,7},{7,6},{8,9},{9,8},{10,11... | collective-permute-start | bytes 1032200 | tf_op jit(solution)/shard_map/ppermute | solution.py:398

commit v2 on v1

--- a/solution.py
+++ b/solution.py
@@ -16,9 +16,11 @@
 T = TILES // SUB
 CHUNKS = LAYERS * SUB
 TAIL = 4
-LEAD = 1
-LAG = 1
-RING = 4
+PIECES = (pl.ds(0, 2), pl.ds(2, T - 2))
+LEAD = 2
+LAG = 2
+RING = 6
+RING0 = 8
 VM = pltpu.VMEM
 ST1, ST2, ST3, AG3, AG2, AG1, ST0, AG0 = range(8)
 
@@ -64,15 +66,36 @@
         b1, b2, b3 = AXES[k]
         return e1 * b1 + e2 * b2 + e3 * b3 + c
 
-    def send_raw(ch):
+    def send_raw(ch, halves=(0, 1)):
         l, rows = where(ch)
-        for half in range(2):
+        for half in halves:
             for k in range(3):
                 side = bit(AXES[k][0]) if half else 1 - bit(AXES[k][0])
                 for q in range(4):
                     j = owner(k, side, q // 2, q % 2, 1 - core)
-                    sem = s0r.at[3 if half else k, lax.rem(ch, RING)]
+                    sem = s0r.at[3 if half else k, lax.rem(ch, RING0)]
                     remote(g[k].at[l, j, rows], D.at[k, ch, 4 * side + q], snd.at[ST0], sem, mate).start()
+
+    def send_first():
+        for piece, rows in enumerate(PIECES):
+            for k in range(3):
+                side = 1 - bit(AXES[k][0])
+                sem = s0r.at[k, 0 if piece else RING0 - 1]
+                for q in range(4):
+                    j = owner(k, side, q // 2, q % 2, 1 - core)
+                    remote(g[k].at[0, j, rows], D.at[k, 0, 4 * side + q, rows], snd.at[ST0], sem, mate).start()
+
+    def stage1_first():
+        loaded(O1.at[0], ld.at[0, 0])
+        for piece, rows in enumerate(PIECES):
+            for k in range(3):
+                b1 = AXES[k][0]
+                base = 4 * (1 - bit(b1))
+                part = D.at[k, 0, pl.ds(base, 4), rows]
+                arrived(part, s0r.at[k, 0 if piece else RING0 - 1])
+                for q in range(4):
+                    add_into(D.at[k, 0, base + q, rows], O1.at[0, k, q, rows], D.at[k, 0, base + q, rows])
+                remote(part, R1.at[0, k, :, rows], snd.at[ST1], rr.at[ST1, 0], flip(me, b1)).start()
 
     def load_own(which, ch):
         l, rows = where(ch)
@@ -101,7 +124,7 @@
         for k in range(3):
             b1, _, _ = AXES[k]
             base = 4 * (1 - bit(b1))
-            arrived(D.at[k, ch, pl.ds(base, 4)], s0r.at[k, ring])
+            arrived(D.at[k, ch, pl.ds(base, 4)], s0r.at[k, lax.rem(ch, RING0)])
 
             def one(q, _):
                 add_into(D.at[k, ch, base + q], O1.at[slot, k, q], D.at[k, ch, base + q])
@@ -112,7 +135,7 @@
 
     def stage2(ch):
         slot, ring = lax.rem(ch, 2), lax.rem(ch, RING)
-        arrived(R1.at[ch], s0r.at[3, ring])
+        arrived(R1.at[ch], s0r.at[3, lax.rem(ch, RING0)])
         arrived(R1.at[ch], rr.at[ST1, ring])
         loaded(O2.at[slot], ld.at[1, slot])
         for k in range(3):
@@ -236,8 +259,11 @@
         pl.semaphore_signal(barrier, inc=1, device_id={"dp": flip(me, b)}, device_id_type=MESH)
     pl.semaphore_wait(barrier, 4)
 
-    for ch in range(LEAD):
-        send_raw(ch)
+    send_first()
+    send_raw(0, (1,))
+    send_raw(1)
+    stage1_first()
+    send_raw(2)
 
     def step(s, _):
         def at(lag, do, *args, start=0):
@@ -247,8 +273,8 @@
             def _():
                 do(*args, ch)
 
-        at(0, stage1)
-        at(-LEAD, send_raw)
+        at(0, stage1, start=1)
+        at(-LEAD, send_raw, start=LEAD + 1)
         at(-1, load_own, 0)
         at(LAG - 1, load_own, 1)
         at(LAG, load_own, 2)
@@ -316,18 +342,18 @@
 
 
 def write_next(*refs):
-    split, both, targets, sem = refs[0], refs[1], refs[5:8], refs[8]
-    put_late(split, both, targets, lax.rem(lax.axis_index("dp"), 2), sem)
-
-
-def write_last(*refs):
     split, both, last, targets, sem = refs[0], refs[1], refs[2], refs[6:9], refs[9]
-    other = 1 - lax.rem(lax.axis_index("dp"), 2)
+    core = lax.rem(lax.axis_index("dp"), 2)
     end, ends = pl.ds(TILES - T, T), []
     for k in range(3):
         far = late_blocks(k, True)
-        ends += [(last.at[k, q], targets[k].at[1, far[2 * q] + other, end]) for q in range(4)]
-    put_late(split, both, targets, other, sem, [(ends, last)])
+        ends += [(last.at[k, q], targets[k].at[1, far[2 * q] + 1 - core, end]) for q in range(4)]
+    put_late(split, both, targets, core, sem, [(ends, last)])
+
+
+def write_last(*refs):
+    split, both, targets, sem = refs[0], refs[1], refs[5:8], refs[8]
+    put_late(split, both, targets, 1 - lax.rem(lax.axis_index("dp"), 2), sem)
 
 
 def tiled(a, parts):
@@ -363,7 +389,7 @@
                 pltpu.VMEM((2, 3, *block), BF16),
                 pltpu.VMEM((2, 3, *block), BF16),
                 pltpu.VMEM((2, 3, *block), BF16),
-                dma((4, RING)),
+                dma((4, RING0)),
                 dma((6, RING)),
                 dma((2,)),
                 dma((8,)),
@@ -399,8 +425,8 @@
         *new_w, m0, m1, m2, v0, v1, v2 = plain(write_early, out_w + out_m, [vmem] * 2, 2, {}, 2 * 10**9)(moments, new_w)
         *new_w, split, both = lax.optimization_barrier((*new_w, split, both))
         mates = [lax.ppermute(one, "dp", [(i, i ^ 1) for i in range(N)]) for one in (split, both)]
-        new_w = plain(write_next, out_w, [any_space] * 2 + [hbm] * 3, 2, {2: 0, 3: 1, 4: 2}, 10**9)(split, both, *new_w)
-        new_w = plain(write_last, out_w, [any_space] * 3 + [hbm] * 3, 3, {3: 0, 4: 1, 5: 2}, 10**9)(*mates, last, *new_w)
+        new_w = plain(write_next, out_w, [any_space] * 3 + [hbm] * 3, 3, {3: 0, 4: 1, 5: 2}, 10**9)(split, both, last, *new_w)
+        new_w = plain(write_last, out_w, [any_space] * 2 + [hbm] * 3, 2, {2: 0, 3: 1, 4: 2}, 10**9)(*mates, *new_w)
         new = (*new_w, m0, m1, m2, v0, v1, v2)
         return (
             *(untiled(one, w.shape) for one, w in zip(new[:3], weights, strict=True)),

time: 190 us -> 191 us (level)
  no operation moved by 1% of the time
where the time goes in v2:
time: 191 us; the launch traced here: 190 us
  Pallas kernels  183 us (96%)
  waiting for transfers between devices  3.79 us (2%)
  starting transfers between devices  2.94 us (2%)
    pallas_call x1, Pallas kernels, step(): pl.pallas_call(kernel, out_shape=[VM((2, 3, *part), F32), VM((3, *whole),...  170 us
    pallas_call x1, Pallas kernels, step(): plain(write_early, out_w + out_m, [vmem] * 2, 2, {}, 2 * 10 ** 9)  10.3 us
  transfers between devices with their start and end apart: 5, of which 3 were waited for; matrix products, arithmetic and copies ran while one was open for 0% of the time, Pallas kernels for 6%

profile of v2, /device:TPU:0, one launch (start us, length us, event | category | flops | bytes accessed | tf_op | source)
XLA Modules:
  0.0 190.4 jit_solution(12489426136403807775)
XLA Ops:
  0.6 170.4 %sum_step_gather.1 = (f32[2,3,2,70,16,128]{5,4,3,2,1,0:T(8,128)S(1)}, bf16[3,2,16,70,16,128]{5,4,3,2,1,0:T(8,128)(2,1)S(1)}, bf16[8,28,16,128]{3,2,1,0:T(8,128)(...) custom-call(bf16[2,16,70,16,128]{4,3,2,1,0:T(8,128)(2,1)} %bitcast.108, ...), custom_call_target="tpu_custom_call" | custom-call | tf_op jit(solution)/shard_map/sum_step_gather/pallas_call | solution.py:377
  171.0 1.5 collective-permute-start
  172.5 0.9 collective-permute-start.1
  173.4 10.3 %shard_map.187 = (bf16[2,16,70,16,128]{4,3,2,1,0:T(8,128)(2,1)}, bf16[2,16,70,16,128]{4,3,2,1,0:T(8,128)(2,1)}, bf16[2,16,70,16,128]{4,3,2,1,0:T(8,128)(2,1)}, f...) custom-call(f32[2,3,2,70,16,128]{5,4,3,2,1,0:T(8,128)S(1)} %get-tupl, ...), custom_call_target="tpu_custom_call" | custom-call | flops 2000000000 | bytes 20000000 | tf_op jit(solution)/shard_map/pallas_call | solution.py:425
  183.8 0.3 collective-permute-done.1.refs_1_
  184.0 0.4 collective-permute-done.refs_0_
  184.4 0.0 collective-permute-start.2
  184.4 0.5 collective-permute-start.3
  184.9 0.0 collective-permute-start.4
  185.0 3.1 %collective-permute-done.4.refs_2_ = bf16[3,4,7,16,128]{4,3,2,1,0:T(8,128)(2,1)S(1)} collective-permute-done((bf16[3,4,7,16,128]{4,3,2,1,0:T(8,128)(2,1)S(1)}, bf16[3,4,7,16,128]{4,3,2,1,0:T(8,128)(2,1)S(1)}, u32[]{:S(2)}, u32[]{:S(2)}) %collective-permute-start.4) | collective-permute-done | bytes 344096 | tf_op jit(solution)/shard_map/ppermute | solution.py:424
  188.1 1.2 shard_map.188
  189.3 0.0 collective-permute-done.3.refs_1_
  189.3 0.0 collective-permute-done.2.refs_0_
  189.3 1.1 shard_map.189
Async XLA Ops:
  171.0 13.4 %collective-permute-start = (bf16[8,28,16,128]{3,2,1,0:T(8,128)(2,1)S(1)}, bf16[8,28,16,128]{3,2,1,0:T(8,128)(2,1)S(1)}, u32[]{:S(2)}, u32[]{:S(2)}) collective-permute-start(bf16[8,28,16,128]{3,2,1,0:T(8,128)(2,1)S(1)} %get-tuple-element.39), channel_id=1, source_target_pairs={{0,4},{1,3},{2,6},{3,1},{4,0},{5,7},{6,2},{7,5},{8,12},{9,11},{10,... | collective-permute-start | bytes 2752520 | tf_op jit(solution)/shard_map/ppermute | solution.py:422
  172.5 11.5 %collective-permute-start.1 = (bf16[4,28,16,128]{3,2,1,0:T(8,128)(2,1)S(1)}, bf16[4,28,16,128]{3,2,1,0:T(8,128)(2,1)S(1)}, u32[]{:S(2)}, u32[]{:S(2)}) collective-permute-start(bf16[4,28,16,128]{3,2,1,0:T(8,128)(2,1)S(1)} %get-tuple-element.40), channel_id=1, source_target_pairs={{0,8},{1,9},{2,10},{3,11},{4,12},{5,13},{6,14},{7,15},{8,0},{9,1},... | collective-permute-start | bytes 1376264 | tf_op jit(solution)/shard_map/ppermute | solution.py:423
  184.4 4.8 %collective-permute-start.2 = (bf16[8,28,16,128]{3,2,1,0:T(8,128)(2,1)S(1)}, bf16[8,28,16,128]{3,2,1,0:T(8,128)(2,1)S(1)}, u32[]{:S(2)}, u32[]{:S(2)}) collective-permute-start(bf16[8,28,16,128]{3,2,1,0:T(8,128)(2,1)S(1)} %collective-permute-done.refs_0_), channel_id=1, source_target_pairs={{0,1},{1,0},{2,3},{3,2},{4,5},{5,4},{6,7},{7,6},{8,9},{9,8},{10,11... | collective-permute-start | bytes 2752520 | tf_op jit(solution)/shard_map/ppermute | solution.py:427
  184.4 4.8 %collective-permute-start.3 = (bf16[4,28,16,128]{3,2,1,0:T(8,128)(2,1)S(1)}, bf16[4,28,16,128]{3,2,1,0:T(8,128)(2,1)S(1)}, u32[]{:S(2)}, u32[]{:S(2)}) collective-permute-start(bf16[4,28,16,128]{3,2,1,0:T(8,128)(2,1)S(1)} %collective-permute-done.1.refs_1_), channel_id=1, source_target_pairs={{0,1},{1,0},{2,3},{3,2},{4,5},{5,4},{6,7},{7,6},{8,9},{9,8},{10,11... | collective-permute-start | bytes 1376264 | tf_op jit(solution)/shard_map/ppermute | solution.py:427
  184.9 3.1 %collective-permute-start.4 = (bf16[3,4,7,16,128]{4,3,2,1,0:T(8,128)(2,1)S(1)}, bf16[3,4,7,16,128]{4,3,2,1,0:T(8,128)(2,1)S(1)}, u32[]{:S(2)}, u32[]{:S(2)}) collective-permute-start(bf16[3,4,7,16,128]{4,3,2,1,0:T(8,128)(2,1)S(1)} %get-tuple-element.43), channel_id=1, source_target_pairs={{0,1},{1,0},{2,3},{3,2},{4,5},{5,4},{6,7},{7,6},{8,9},{9,8},{10,11... | collective-permute-start | bytes 1032200 | tf_op jit(solution)/shard_map/ppermute | solution.py:424

commit v3 on v2

--- a/solution.py
+++ b/solution.py
@@ -19,10 +19,9 @@
 PIECES = (pl.ds(0, 2), pl.ds(2, T - 2))
 LEAD = 2
 LAG = 2
-RING = 6
-RING0 = 8
+RING, RING1, NEAR = 4, 6, 8
 VM = pltpu.VMEM
-ST1, ST2, ST3, AG3, AG2, AG1, ST0, AG0 = range(8)
+ST1, ST2, ST3, AG3, AG2, AG1, _, AG0 = range(8)
 
 
 def add_into(dst, *srcs):
@@ -38,7 +37,7 @@
     split, both, mate_part = refs[14:17]
     wo = [new_w.at[k] for k in range(3)]
     mo, vo = ([moments.at[i, k] for k in range(3)] for i in range(2))
-    D, R1, R2, R3, O1, O2, O3, O4, W, s0r, rr, a0r, snd, ld, mv = refs[17:]
+    D, R1, R2, R3, O1, O2, O3, O4, W, far, near, early, rr, a0r, snd, ld, mv = refs[17:]
     me = lax.axis_index("dp")
 
     def bit(b):
@@ -54,10 +53,13 @@
         return pltpu.make_async_remote_copy(src, dst, send, recv, device_id={"dp": to}, device_id_type=MESH)
 
     def arrived(ref, sem):
-        remote(ref, ref, snd.at[ST0], sem, mate).wait_recv()
+        remote(ref, ref, snd.at[0], sem, mate).wait_recv()
 
     def loaded(ref, sem):
         pltpu.make_async_copy(ref, ref, sem).wait()
+
+    def came(stage, ch):
+        return rr.at[lax.rem(ch, RING1) if stage == ST1 else RING1 + RING * (stage - 1) + lax.rem(ch, RING)]
 
     def where(ch):
         return ch // SUB, pl.ds(lax.rem(ch, SUB) * T, T)
@@ -73,17 +75,17 @@
                 side = bit(AXES[k][0]) if half else 1 - bit(AXES[k][0])
                 for q in range(4):
                     j = owner(k, side, q // 2, q % 2, 1 - core)
-                    sem = s0r.at[3 if half else k, lax.rem(ch, RING0)]
-                    remote(g[k].at[l, j, rows], D.at[k, ch, 4 * side + q], snd.at[ST0], sem, mate).start()
+                    sem = near.at[lax.rem(ch, NEAR)] if half else far.at[lax.rem(ch, RING)]
+                    remote(g[k].at[l, j, rows], D.at[k, ch, 4 * side + q], snd.at[0], sem, mate).start()
 
     def send_first():
         for piece, rows in enumerate(PIECES):
             for k in range(3):
                 side = 1 - bit(AXES[k][0])
-                sem = s0r.at[k, 0 if piece else RING0 - 1]
+                sem = early.at[piece, k]
                 for q in range(4):
                     j = owner(k, side, q // 2, q % 2, 1 - core)
-                    remote(g[k].at[0, j, rows], D.at[k, 0, 4 * side + q, rows], snd.at[ST0], sem, mate).start()
+                    remote(g[k].at[0, j, rows], D.at[k, 0, 4 * side + q, rows], snd.at[0], sem, mate).start()
 
     def stage1_first():
         loaded(O1.at[0], ld.at[0, 0])
@@ -92,10 +94,10 @@
                 b1 = AXES[k][0]
                 base = 4 * (1 - bit(b1))
                 part = D.at[k, 0, pl.ds(base, 4), rows]
-                arrived(part, s0r.at[k, 0 if piece else RING0 - 1])
+                arrived(part, early.at[piece, k])
                 for q in range(4):
                     add_into(D.at[k, 0, base + q, rows], O1.at[0, k, q, rows], D.at[k, 0, base + q, rows])
-                remote(part, R1.at[0, k, :, rows], snd.at[ST1], rr.at[ST1, 0], flip(me, b1)).start()
+                remote(part, R1.at[0, k, :, rows], snd.at[0], came(ST1, 0), flip(me, b1)).start()
 
     def load_own(which, ch):
         l, rows = where(ch)
@@ -119,24 +121,24 @@
                 pltpu.make_async_copy(w[k].at[l, me, rows], W.at[slot, k], ld.at[4, slot]).start()
 
     def stage1(ch):
-        slot, ring = lax.rem(ch, 2), lax.rem(ch, RING)
+        slot = lax.rem(ch, 2)
+        arrived(R1.at[ch], far.at[lax.rem(ch, RING)])
         loaded(O1.at[slot], ld.at[0, slot])
         for k in range(3):
             b1, _, _ = AXES[k]
             base = 4 * (1 - bit(b1))
-            arrived(D.at[k, ch, pl.ds(base, 4)], s0r.at[k, lax.rem(ch, RING0)])
 
             def one(q, _):
                 add_into(D.at[k, ch, base + q], O1.at[slot, k, q], D.at[k, ch, base + q])
                 return 0
 
             lax.fori_loop(0, 4, one, 0)
-            remote(D.at[k, ch, pl.ds(base, 4)], R1.at[ch, k], snd.at[ST1], rr.at[ST1, ring], flip(me, b1)).start()
+            remote(D.at[k, ch, pl.ds(base, 4)], R1.at[ch, k], snd.at[0], came(ST1, ch), flip(me, b1)).start()
 
     def stage2(ch):
-        slot, ring = lax.rem(ch, 2), lax.rem(ch, RING)
-        arrived(R1.at[ch], s0r.at[3, lax.rem(ch, RING0)])
-        arrived(R1.at[ch], rr.at[ST1, ring])
+        slot = lax.rem(ch, 2)
+        arrived(R1.at[ch], near.at[lax.rem(ch, NEAR)])
+        arrived(R1.at[ch], came(ST1, ch))
         loaded(O2.at[slot], ld.at[1, slot])
         for k in range(3):
             b1, b2, _ = AXES[k]
@@ -148,35 +150,35 @@
                 return 0
 
             lax.fori_loop(0, 2, one, 0)
-            remote(D.at[k, ch, pl.ds(base, 2)], R2.at[ch, k], snd.at[ST2], rr.at[ST2, ring], flip(me, b2)).start()
+            remote(D.at[k, ch, pl.ds(base, 2)], R2.at[ch, k], snd.at[0], came(ST2, ch), flip(me, b2)).start()
 
     def stage3(ch):
-        slot, ring = lax.rem(ch, 2), lax.rem(ch, RING)
-        arrived(R2.at[ch], rr.at[ST2, ring])
+        slot = lax.rem(ch, 2)
+        arrived(R2.at[ch], came(ST2, ch))
         loaded(O3.at[slot], ld.at[2, slot])
         for k in range(3):
             b1, b2, b3 = AXES[k]
             m1, m2, n3 = bit(b1), bit(b2), 1 - bit(b3)
             mine = D.at[k, ch, 4 * m1 + 2 * m2 + n3]
             add_into(mine, O3.at[slot, k], mine, R1.at[ch, k, 2 * m2 + n3], R2.at[ch, k, n3])
-            remote(mine, R3.at[ch, k], snd.at[ST3], rr.at[ST3, ring], flip(me, b3)).start()
+            remote(mine, R3.at[ch, k], snd.at[0], came(ST3, ch), flip(me, b3)).start()
 
     def give(k, ch, stage, blocks, to):
         l, rows = where(ch)
-        recv = a0r.at[lax.min(ch // TAIL, 1)] if stage == AG0 else rr.at[stage, lax.rem(ch, RING)]
+        recv = a0r.at[lax.min(ch // TAIL, 1)] if stage == AG0 else came(stage, ch)
         for j in blocks:
             part = wo[k].at[l, j, rows]
-            remote(part, part, snd.at[stage], recv, to).start()
+            remote(part, part, snd.at[1], recv, to).start()
 
     def update(ch):
         l, rows = where(ch)
-        slot, ring = lax.rem(ch, 2), lax.rem(ch, RING)
+        slot = lax.rem(ch, 2)
 
         @pl.when(ch == 0)
         def _():
             loaded(moments, mv.at[0])
 
-        arrived(R3.at[ch], rr.at[ST3, ring])
+        arrived(R3.at[ch], came(ST3, ch))
         loaded(O4.at[slot], ld.at[3, slot])
         loaded(W.at[slot], ld.at[4, slot])
         for k in range(3):
@@ -196,7 +198,7 @@
             give(k, ch, AG0, (me,), mate)
 
     def double3(ch):
-        arrived(R3.at[ch], rr.at[AG3, lax.rem(ch, RING)])
+        arrived(R3.at[ch], came(AG3, ch))
         for k in range(3):
             _, b2, b3 = AXES[k]
             got = flip(me, b3)
@@ -204,7 +206,7 @@
             give(k, ch, AG0, (got,), mate)
 
     def double2(ch):
-        arrived(R2.at[ch], rr.at[AG2, lax.rem(ch, RING)])
+        arrived(R2.at[ch], came(AG2, ch))
         for k in range(3):
             b1, b2, b3 = AXES[k]
             held = (me, flip(me, b3))
@@ -218,7 +220,7 @@
 
     def double1(ch):
         l, rows = where(ch)
-        arrived(R1.at[ch], rr.at[AG1, lax.rem(ch, RING)])
+        arrived(R1.at[ch], came(AG1, ch))
         for k in range(3):
             b1, b2, b3 = AXES[k]
             held = (me, flip(me, b3))
@@ -291,17 +293,8 @@
     lax.fori_loop(0, CHUNKS + LAG + 5, step, 0)
 
     arrived(new_w.at[:, :, pl.ds(0, 7), pl.ds(0, 62)], a0r.at[1])
-    for stage, sent in (
-        (ST0, D),
-        (ST1, R1),
-        (ST2, R2),
-        (ST3, R3),
-        (AG3, R3),
-        (AG2, R2),
-        (AG1, R1.at[pl.ds(0, CHUNKS - TAIL)]),
-        (AG0, D.at[:, :, pl.ds(0, 7)]),
-    ):
-        remote(sent, sent, snd.at[stage], a0r.at[0], mate).wait_send()
+    for i, sent in enumerate((new_w.at[:, :, pl.ds(0, 15)], new_w.at[:, :, pl.ds(0, 14), pl.ds(0, 66)])):
+        remote(sent, sent, snd.at[i], a0r.at[0], mate).wait_send()
 
 
 def run_copies(groups, sem):
@@ -389,10 +382,12 @@
                 pltpu.VMEM((2, 3, *block), BF16),
                 pltpu.VMEM((2, 3, *block), BF16),
                 pltpu.VMEM((2, 3, *block), BF16),
-                dma((4, RING0)),
-                dma((6, RING)),
+                dma((RING,)),
+                dma((NEAR,)),
+                dma((2, 3)),
+                dma((RING1 + 5 * RING,)),
                 dma((2,)),
-                dma((8,)),
+                dma((2,)),
                 dma((5, 2)),
                 dma((1,)),
             ],

time: 191 us -> 190 us (level)
  no operation moved by 1% of the time
where the time goes in v3:
time: 190 us
  Pallas kernels  183 us (96%)
  waiting for transfers between devices  3.79 us (2%)
  starting transfers between devices  2.94 us (2%)
    pallas_call x1, Pallas kernels, step(): pl.pallas_call(kernel, out_shape=[VM((2, 3, *part), F32), VM((3, *whole),...  170 us
    pallas_call x1, Pallas kernels, step(): plain(write_early, out_w + out_m, [vmem] * 2, 2, {}, 2 * 10 ** 9)  10.3 us
  transfers between devices with their start and end apart: 5, of which 3 were waited for; matrix products, arithmetic and copies ran while one was open for 0% of the time, Pallas kernels for 6%

profile of v3, /device:TPU:0, one launch (start us, length us, event | category | flops | bytes accessed | tf_op | source)
XLA Modules:
  0.0 190.1 jit_solution(18411439271197224950)
XLA Ops:
  0.6 170.1 %sum_step_gather.1 = (f32[2,3,2,70,16,128]{5,4,3,2,1,0:T(8,128)S(1)}, bf16[3,2,16,70,16,128]{5,4,3,2,1,0:T(8,128)(2,1)S(1)}, bf16[8,28,16,128]{3,2,1,0:T(8,128)(...) custom-call(bf16[2,16,70,16,128]{4,3,2,1,0:T(8,128)(2,1)} %bitcast.108, ...), custom_call_target="tpu_custom_call" | custom-call | tf_op jit(solution)/shard_map/sum_step_gather/pallas_call | solution.py:370
  170.7 1.5 collective-permute-start
  172.3 0.9 collective-permute-start.1
  173.2 10.3 %shard_map.187 = (bf16[2,16,70,16,128]{4,3,2,1,0:T(8,128)(2,1)}, bf16[2,16,70,16,128]{4,3,2,1,0:T(8,128)(2,1)}, bf16[2,16,70,16,128]{4,3,2,1,0:T(8,128)(2,1)}, f...) custom-call(f32[2,3,2,70,16,128]{5,4,3,2,1,0:T(8,128)S(1)} %get-tupl, ...), custom_call_target="tpu_custom_call" | custom-call | flops 2000000000 | bytes 20000000 | tf_op jit(solution)/shard_map/pallas_call | solution.py:420
  183.5 0.3 collective-permute-done.1.refs_1_
  183.8 0.4 collective-permute-done.refs_0_
  184.2 0.0 collective-permute-start.2
  184.2 0.5 collective-permute-start.3
  184.7 0.0 collective-permute-start.4
  184.7 3.1 %collective-permute-done.4.refs_2_ = bf16[3,4,7,16,128]{4,3,2,1,0:T(8,128)(2,1)S(1)} collective-permute-done((bf16[3,4,7,16,128]{4,3,2,1,0:T(8,128)(2,1)S(1)}, bf16[3,4,7,16,128]{4,3,2,1,0:T(8,128)(2,1)S(1)}, u32[]{:S(2)}, u32[]{:S(2)}) %collective-permute-start.4) | collective-permute-done | bytes 344096 | tf_op jit(solution)/shard_map/ppermute | solution.py:419
  187.8 1.2 shard_map.188
  189.0 0.0 collective-permute-done.3.refs_1_
  189.0 0.0 collective-permute-done.2.refs_0_
  189.0 1.1 shard_map.189
Async XLA Ops:
  170.7 13.4 %collective-permute-start = (bf16[8,28,16,128]{3,2,1,0:T(8,128)(2,1)S(1)}, bf16[8,28,16,128]{3,2,1,0:T(8,128)(2,1)S(1)}, u32[]{:S(2)}, u32[]{:S(2)}) collective-permute-start(bf16[8,28,16,128]{3,2,1,0:T(8,128)(2,1)S(1)} %get-tuple-element.39), channel_id=1, source_target_pairs={{0,4},{1,3},{2,6},{3,1},{4,0},{5,7},{6,2},{7,5},{8,12},{9,11},{10,... | collective-permute-start | bytes 2752520 | tf_op jit(solution)/shard_map/ppermute | solution.py:417
  172.3 11.5 %collective-permute-start.1 = (bf16[4,28,16,128]{3,2,1,0:T(8,128)(2,1)S(1)}, bf16[4,28,16,128]{3,2,1,0:T(8,128)(2,1)S(1)}, u32[]{:S(2)}, u32[]{:S(2)}) collective-permute-start(bf16[4,28,16,128]{3,2,1,0:T(8,128)(2,1)S(1)} %get-tuple-element.40), channel_id=1, source_target_pairs={{0,8},{1,9},{2,10},{3,11},{4,12},{5,13},{6,14},{7,15},{8,0},{9,1},... | collective-permute-start | bytes 1376264 | tf_op jit(solution)/shard_map/ppermute | solution.py:418
  184.2 4.8 %collective-permute-start.2 = (bf16[8,28,16,128]{3,2,1,0:T(8,128)(2,1)S(1)}, bf16[8,28,16,128]{3,2,1,0:T(8,128)(2,1)S(1)}, u32[]{:S(2)}, u32[]{:S(2)}) collective-permute-start(bf16[8,28,16,128]{3,2,1,0:T(8,128)(2,1)S(1)} %collective-permute-done.refs_0_), channel_id=1, source_target_pairs={{0,1},{1,0},{2,3},{3,2},{4,5},{5,4},{6,7},{7,6},{8,9},{9,8},{10,11... | collective-permute-start | bytes 2752520 | tf_op jit(solution)/shard_map/ppermute | solution.py:422
  184.2 4.8 %collective-permute-start.3 = (bf16[4,28,16,128]{3,2,1,0:T(8,128)(2,1)S(1)}, bf16[4,28,16,128]{3,2,1,0:T(8,128)(2,1)S(1)}, u32[]{:S(2)}, u32[]{:S(2)}) collective-permute-start(bf16[4,28,16,128]{3,2,1,0:T(8,128)(2,1)S(1)} %collective-permute-done.1.refs_1_), channel_id=1, source_target_pairs={{0,1},{1,0},{2,3},{3,2},{4,5},{5,4},{6,7},{7,6},{8,9},{9,8},{10,11... | collective-permute-start | bytes 1376264 | tf_op jit(solution)/shard_map/ppermute | solution.py:422
  184.7 3.1 %collective-permute-start.4 = (bf16[3,4,7,16,128]{4,3,2,1,0:T(8,128)(2,1)S(1)}, bf16[3,4,7,16,128]{4,3,2,1,0:T(8,128)(2,1)S(1)}, u32[]{:S(2)}, u32[]{:S(2)}) collective-permute-start(bf16[3,4,7,16,128]{4,3,2,1,0:T(8,128)(2,1)S(1)} %get-tuple-element.43), channel_id=1, source_target_pairs={{0,1},{1,0},{2,3},{3,2},{4,5},{5,4},{6,7},{7,6},{8,9},{9,8},{10,11... | collective-permute-start | bytes 1032200 | tf_op jit(solution)/shard_map/ppermute | solution.py:419
